TPU v7x, 32 devices: a whole 2x2x4 slice. The times are simulated.
32 devices in a mesh: gx: 8 (over z, y), gy: 4 (over x, core).
Axes of the slice: x: 2, y: 2, z: 4, core: 2. Of those that a mesh axis runs over, the one named last changes fastest.
Arguments:
- table: float32 [4, 65536, 128], P(None, 'gx'), may hold values from -2.1 to 2.1
- lookup_owner: int32 [4, 8192, 16, 1], P(None, ('gx', 'gy')), may hold values from 0 to 7; in each aligned block of 4096 rows (0 to 4095, 4096 to 8191, ..., all dimensions but the last counted through in order) at most 1024 rows name the same one
- lookup_row: int32 [4, 8192, 16], P(None, ('gx', 'gy')), may hold values from 0 to 8191
- bag_length: int32 [4, 8192], P(None, ('gx', 'gy')), may hold values from 1 to 16
- top_in: bfloat16 [512, 8192], P(None, 'gy'), may hold values from -0.25 to 0.25
- top_bias: float32 [8192], P('gy'), may hold values from -3 to 3
- top_out: bfloat16 [8192, 1024], P('gy'), may hold values from -0.0625 to 0.0625
Outputs:
- scored: bfloat16 [8192, 1024], P(('gx', 'gy'))
Inputs may be any that keep to these rules, and one draw needn't show every extreme that they name: `lookup_owner`: in every aligned block of 4096 entries (the lookups of one table from the samples of one device) no owner is named more than 1024 times; some blocks reach 1024.
All inputs are finite; a program needn't handle non-finite values.
Results may differ from a plain program's by a relative error of at most 0.0057.
Values may be sent and summed in bfloat16 or wider, within the bound.
A program may use at most 128 MiB of HBM per device.

v0:
```python
import functools
import jax
import jax.numpy as jnp
from jax import lax
from jax.experimental import pallas as pl
from jax.experimental.pallas import tpu as pltpu
from jax.sharding import PartitionSpec as P

BIG = 2**31 - 1
MESH = pl.DeviceIdType.MESH


def log2(n):
    return n.bit_length() - 1


def sort_kernel(rows_dev, owner_ref, row_ref, bag_ref, rows_ref, bags_ref, mine, outbox, held, send_sem, recv_sem):
    owners = held.shape[0]
    me = lax.axis_index("gx")
    barrier = pltpu.get_barrier_semaphore()
    for k in range(1, owners):
        pl.semaphore_signal(barrier, inc=1, device_id={"gx": lax.rem(me + k, owners)}, device_id_type=MESH)
    tables, bag_size, samples = owner_ref.shape
    owner = owner_ref[...]
    slot = lax.broadcasted_iota(jnp.int32, owner.shape, 1)
    sample = lax.broadcasted_iota(jnp.int32, owner.shape, 2)
    live = slot < bag_ref[...][:, None, :]
    key = jnp.where(live, (owner * samples + sample) * rows_dev + row_ref[...], BIG)
    count = bag_size * samples
    groups = count // 1024
    parts = []
    for t in range(tables):
        for c in range(samples // 128):
            for r in range(bag_size // 8):
                parts.append(key[t, r * 8 : r * 8 + 8, c * 128 : c * 128 + 128])
    lane = lax.broadcasted_iota(jnp.int32, (8, 128), 1)
    sub = lax.broadcasted_iota(jnp.int32, (8, 128), 0)
    place = lane * 8 + sub
    bits = log2(count)
    span = samples * rows_dev

    before = []
    for o in range(1, owners):
        for t in range(tables):
            tally = jnp.zeros((8, 128), jnp.int32)
            for g in range(groups):
                tally += (parts[t * groups + g] < o * span).astype(jnp.int32)
            before.append(jnp.sum(tally, axis=0, keepdims=True))
    before = jnp.sum(jnp.concatenate(before, axis=0), axis=1, keepdims=True)

    for k in range(1, bits + 1):
        for j in range(k - 1, -1, -1):
            d = 1 << j
            new = [None] * len(parts)
            for v in range(len(parts)):
                g = v % groups
                if d >= 1024:
                    gd = d // 1024
                    if g & gd:
                        continue
                    w = v + gd
                    low = jnp.minimum(parts[v], parts[w])
                    high = jnp.maximum(parts[v], parts[w])
                    up = ((g * 1024) >> k) & 1 == 0
                    new[v], new[w] = (low, high) if up else (high, low)
                    continue
                x = parts[v]
                if d < 8:
                    a, b = pltpu.roll(x, 8 - d, 0), pltpu.roll(x, d, 0)
                else:
                    s = d // 8
                    a, b = pltpu.roll(x, 128 - s, 1), pltpu.roll(x, s, 1)
                first = (place & d) == 0
                other = jnp.where(first, a, b)
                if (1 << k) >= 1024:
                    up = ((g * 1024) >> k) & 1 == 0
                    take_low = first if up else jnp.logical_not(first)
                else:
                    take_low = ((place >> k) ^ (place >> j)) & 1 == 0
                new[v] = jnp.where(take_low, jnp.minimum(x, other), jnp.maximum(x, other))
            parts = new
    stride = mine.shape[0] // tables
    for t in range(tables):
        for g in range(stride // 8):
            at = t * stride + g * 8
            mine[at : at + 8, :] = parts[t * groups + g] if g < groups else jnp.full((8, 128), BIG, jnp.int32)

    for o in range(owners):
        for t in range(tables):
            if o == 0:
                x = mine[t * stride : t * stride + 8, :]
            else:
                off = before[(o - 1) * tables + t, 0]
                low = off & 7

                def columns(first):
                    at = t * stride + ((first >> 7) << 3)
                    left = 128 - (first & 127)
                    turn = left & 127
                    p = pltpu.roll(mine[pl.ds(at, 8), :], turn, 1)
                    q = pltpu.roll(mine[pl.ds(at + 8, 8), :], turn, 1)
                    return pltpu.roll(jnp.where(lane < left, p, q), (8 - low) & 7, 0)

                x = jnp.where(sub < 8 - low, columns(off >> 3), columns((off >> 3) + 1))
            x = x - o * span
            ours = jnp.logical_and(x >= 0, x < span)
            outbox[o, t * 8 : t * 8 + 8, :] = jnp.where(ours, x, span)

    pl.semaphore_wait(barrier, owners - 1)
    copies = []
    for k in range(1, owners):
        to = lax.rem(me + k, owners)
        copies.append(
            pltpu.make_async_remote_copy(
                src_ref=outbox.at[to],
                dst_ref=held.at[me],
                send_sem=send_sem.at[k],
                recv_sem=recv_sem.at[k],
                device_id={"gx": to},
                device_id_type=MESH,
            )
        )
        copies[-1].start()

    def split(source, get):
        for t in range(tables):
            x = get(pl.ds(t * 8, 8))
            rows_ref[:, pl.ds(source * tables + t, 1), :] = ((x & (rows_dev - 1)) + t * rows_dev)[:, None, :]
            bags_ref[source, t * 8 : t * 8 + 8, :] = x >> log2(rows_dev)

    split(me, lambda at: outbox[me, at, :])
    for k in range(1, owners):
        source = lax.rem(me - k + owners, owners)
        copies[k - 1].wait_recv()
        split(source, lambda at: held[source, at, :])
    for copy in copies:
        copy.wait_send()


def exchange_kernel(part_ref, top_in_ref, bias_ref, top_out_ref, out_ref, from_y, sum_y, from_z, feat, w_in, w_out, hid, near_out, near_in, far_out, w_send, far_in, wsem, ysem, yrec, zsem, zrec, gsem, grec, rsem, rrec, nsem, nrec, fsem, frec):
    owners, samples, width = part_ref.shape
    inner = from_y.shape[0] + 1
    outer = owners // inner
    chips = far_in.shape[0] + 1
    me, mine = lax.axis_index("gx"), lax.axis_index("gy")
    z, y = me // inner, lax.rem(me, inner)
    chip, core = mine // 2, lax.rem(mine, 2)
    partner = chip * 2 + 1 - core
    loads = [
        pltpu.make_async_copy(top_in_ref, w_in, wsem.at[0]),
        pltpu.make_async_copy(top_out_ref, w_out, wsem.at[1]),
    ]
    for load in loads:
        load.start()

    def gx_at(index):
        return {"gx": index}

    def gy_at(index):
        return {"gy": index}

    def remote(src, dst, send, recv, device):
        return pltpu.make_async_remote_copy(
            src_ref=src, dst_ref=dst, send_sem=send, recv_sem=recv, device_id=device, device_id_type=MESH
        )

    def y_at(d):
        return z * inner + lax.rem(y + d, inner)

    def z_at(d):
        return lax.rem(z + d, outer) * inner + y

    def chip_at(d):
        return lax.rem(chip + d, chips) * 2 + core

    peers = [gx_at(y_at(d)) for d in range(1, inner)]
    peers += [gx_at(z_at(d)) for d in range(1, outer)]
    peers += [gy_at(partner)] + [gy_at(chip_at(d)) for d in range(1, chips)]
    barrier = pltpu.get_barrier_semaphore()
    for peer in peers:
        pl.semaphore_signal(barrier, inc=1, device_id=peer, device_id_type=MESH)
    pl.semaphore_wait(barrier, len(peers))

    sends = []
    order = sorted(range(1, outer), key=lambda d: -min(d, outer - d)) + [0]
    y_copies = {}
    for dz in order:
        for d in range(1, inner):
            block = lax.rem(z + dz, outer)
            copy = remote(
                part_ref.at[block * inner + lax.rem(y + d, inner)],
                from_y.at[d - 1, dz],
                ysem.at[d - 1, dz],
                yrec.at[d - 1, dz],
                gx_at(y_at(d)),
            )
            copy.start()
            y_copies[dz, d] = copy
            sends.append(copy)
    step = 64
    z_copies = []
    for dz in order:
        block = lax.rem(z + dz, outer)
        for d in range(1, inner):
            y_copies[dz, d].wait_recv()

        @pl.loop(0, samples // step)
        def _(i):
            rows = pl.ds(pl.multiple_of(i * step, step), step)
            total = part_ref[block * inner + y, rows, :].astype(jnp.float32)
            for d in range(1, inner):
                total += from_y[d - 1, dz, rows, :].astype(jnp.float32)
            sum_y[dz, rows, :] = total.astype(sum_y.dtype)

        if dz:
            copy = remote(sum_y.at[dz], from_z.at[dz - 1], zsem.at[dz - 1], zrec.at[dz - 1], gx_at(z_at(dz)))
            copy.start()
            z_copies.append(copy)
    for copy in z_copies:
        copy.wait_recv()

    @pl.loop(0, samples // step)
    def _(i):
        rows = pl.ds(pl.multiple_of(i * step, step), step)
        total = sum_y[0, rows, :].astype(jnp.float32)
        for d in range(1, outer):
            total += from_z[d - 1, rows, :].astype(jnp.float32)
        feat[0, rows, :] = total.astype(feat.dtype)

    far = []
    for d in range(1, chips):
        copy = remote(feat.at[0], feat.at[2 * (chips - d)], gsem.at[d], grec.at[chips - d], gy_at(chip_at(d)))
        copy.start()
        far.append(copy)
    near = [remote(feat.at[0], feat.at[1], rsem.at[0], rrec.at[0], gy_at(partner))]
    near[0].start()
    for load in loads:
        load.wait()
    tile = 512
    hidden, outs = w_in.shape[1], w_out.shape[1]

    def scores(index, put):
        @pl.loop(0, hidden // tile)
        def _(i):
            cols = pl.ds(pl.multiple_of(i * tile, tile), tile)
            pre = jnp.dot(feat[index], w_in[:, cols], preferred_element_type=jnp.float32) + bias_ref[:, cols]
            hid[:, cols] = jnp.maximum(pre, 0.0).astype(hid.dtype)

        @pl.loop(0, outs // tile)
        def _(i):
            cols = pl.ds(pl.multiple_of(i * tile, tile), tile)
            put(cols, jnp.dot(hid[...], w_out[:, cols], preferred_element_type=jnp.float32))

    def to_partner(d):
        def put(cols, value):
            near_out[d, :, cols] = value.astype(near_out.dtype)

        scores(2 * d + 1, put)
        copy = remote(near_out.at[d], near_in.at[d], nsem.at[d], nrec.at[d], gy_at(partner))
        copy.start()
        return copy

    def kept(d):
        def put(cols, value):
            far_out[d, :, cols] = value

        scores(2 * d, put)

    last = []
    kept(0)
    near[0].wait_recv()
    last.append(to_partner(0))
    for d in range(1, chips):
        far[chips - 1 - d].wait_recv()
        copy = remote(feat.at[2 * d], feat.at[2 * d + 1], rsem.at[d], rrec.at[d], gy_at(partner))
        copy.start()
        near.append(copy)
        kept(d)
        copy.wait_recv()
        last.append(to_partner(d))
    far_copies = []
    for d in range(1, chips):
        last[d].wait_recv()

        @pl.loop(0, samples // step)
        def _(i):
            rows = pl.ds(pl.multiple_of(i * step, step), step)
            total = far_out[d, rows, :] + near_in[d, rows, :].astype(jnp.float32)
            w_send[d - 1, rows, :] = total.astype(w_send.dtype)

        copy = remote(w_send.at[d - 1], far_in.at[d - 1], fsem.at[d - 1], frec.at[d - 1], gy_at(chip_at(d)))
        copy.start()
        far_copies.append(copy)
    last[0].wait_recv()
    for copy in far_copies:
        copy.wait_recv()

    @pl.loop(0, samples // step)
    def _(i):
        rows = pl.ds(pl.multiple_of(i * step, step), step)
        total = far_out[0, rows, :] + near_in[0, rows, :].astype(jnp.float32)
        for d in range(1, chips):
            total += far_in[d - 1, rows, :].astype(jnp.float32)
        out_ref[rows, :] = total.astype(out_ref.dtype)

    for copy in sends + z_copies + far + near + last + far_copies:
        copy.wait_send()


def pool_kernel(rows_hbm, bags_ref, table_ref, out_ref, tab, stage, rows, lives, tsem, ksem):
    tables, rows_dev, emb = table_ref.shape
    sources, samples, _ = out_ref.shape
    items = sources * tables
    loads = [
        pltpu.make_async_copy(table_ref.at[t], tab.at[pl.ds(t * rows_dev, rows_dev)], tsem.at[t])
        for t in range(tables)
    ]
    keys = [
        pltpu.make_async_copy(rows_hbm.at[pl.ds(u * items * 128, items * 128)], rows[u], ksem.at[u])
        for u in range(8)
    ]
    for copy in keys + loads:
        copy.start()
    tallies = []
    for i in range(items):
        live = (bags_ref[i // tables, i % tables * 8 : i % tables * 8 + 8, :] < samples).astype(jnp.int32)
        tallies.append(jnp.sum(live, axis=0, keepdims=True))
    tallies = jnp.sum(jnp.concatenate(tallies, axis=0), axis=1, keepdims=True)
    for i in range(items):
        lives[i] = tallies[i, 0]
    stage[...] = jnp.zeros_like(stage)
    place = lax.broadcasted_iota(jnp.int32, (samples, 128), 0)
    for copy in keys:
        copy.wait()

    for t in range(tables):
        loads[t].wait()

        @pl.loop(0, sources)
        def _(s):
            item = s * tables + t

            @pl.loop(0, (lives[item] + 63) // 64)
            def _(i):
                for k in range(8):
                    key = item * 128 + i * 8 + k
                    for u in range(8):
                        stage[pl.ds(s * 1024 + i * 8 + u * 128 + k, 1), :] = tab[pl.ds(rows[u][key], 1), :]

        @pl.loop(0, sources // 4)
        def _(i):
            for k in range(4):
                s = i * 4 + k
                picks = []
                for u in range(8):
                    bag = bags_ref[s, t * 8 + u : t * 8 + u + 1, :]
                    picks.append(jnp.where(place == bag, 1.0, 0.0).astype(jnp.bfloat16))
                held = stage[pl.ds(pl.multiple_of(s * 1024, 1024), 1024), :].astype(jnp.bfloat16)
                total = jnp.dot(jnp.concatenate(picks, axis=1), held, preferred_element_type=jnp.float32)
                out_ref[s, :, t * emb : (t + 1) * emb] = total.astype(out_ref.dtype)


def local(table, lookup_owner, lookup_row, bag_length, top_in, top_bias, top_out):
    owners = lax.axis_size("gx")
    me = lax.axis_index("gx")
    tables, samples, bag_size = lookup_row.shape
    rows_dev = table.shape[1]
    emb = table.shape[2]
    count = samples * bag_size
    assert 2 * count // owners <= 1024
    vmem = pl.BlockSpec(memory_space=pltpu.VMEM)
    anywhere = pl.BlockSpec(memory_space=pl.ANY)

    items = owners * tables
    windows = pltpu.VMEM((owners, tables * 8, 128), jnp.int32)
    rows, bags = pl.pallas_call(
        functools.partial(sort_kernel, rows_dev),
        out_shape=(
            jax.ShapeDtypeStruct((8, items, 128), jnp.int32),
            jax.ShapeDtypeStruct((owners, tables * 8, 128), jnp.int32),
        ),
        scratch_shapes=[
            pltpu.VMEM((tables * (count // 128 + 16), 128), jnp.int32),
            windows,
            windows,
            pltpu.SemaphoreType.DMA((owners,)),
            pltpu.SemaphoreType.DMA((owners,)),
        ],
        compiler_params=pltpu.CompilerParams(collective_id=0, has_side_effects=True),
        name="sort_keys",
    )(
        jnp.transpose(lookup_owner[..., 0], (0, 2, 1)),
        jnp.transpose(lookup_row, (0, 2, 1)),
        bag_length,
    )
    partial = pl.pallas_call(
        pool_kernel,
        out_shape=jax.ShapeDtypeStruct((owners, samples, tables * emb), jnp.bfloat16),
        in_specs=[anywhere, vmem, anywhere],
        out_specs=vmem,
        scratch_shapes=[
            pltpu.VMEM((tables * rows_dev, emb), jnp.float32),
            pltpu.VMEM((owners * 1024, emb), jnp.float32),
            [pltpu.SMEM((items * 128,), jnp.int32) for _ in range(8)],
            pltpu.SMEM((items,), jnp.int32),
            pltpu.SemaphoreType.DMA((tables,)),
            pltpu.SemaphoreType.DMA((8,)),
        ],
        name="pool",
    )(rows.reshape(-1), bags, table)
    inner = max(1, owners // 4)
    outer = owners // inner
    chips = lax.axis_size("gy") // 2
    width = tables * emb
    hidden, outs = top_out.shape
    bf16, dma = jnp.bfloat16, pltpu.SemaphoreType.DMA
    return pl.pallas_call(
        exchange_kernel,
        out_shape=jax.ShapeDtypeStruct((samples, outs), bf16),
        in_specs=[vmem, pl.BlockSpec(memory_space=pl.ANY), vmem, pl.BlockSpec(memory_space=pl.ANY)],
        out_specs=vmem,
        scratch_shapes=[
            pltpu.VMEM((inner - 1, outer, samples, width), bf16),
            pltpu.VMEM((outer, samples, width), bf16),
            pltpu.VMEM((outer - 1, samples, width), bf16),
            pltpu.VMEM((2 * chips, samples, width), bf16),
            pltpu.VMEM((width, hidden), bf16),
            pltpu.VMEM((hidden, outs), bf16),
            pltpu.VMEM((samples, hidden), bf16),
            pltpu.VMEM((chips, samples, outs), bf16),
            pltpu.VMEM((chips, samples, outs), bf16),
            pltpu.VMEM((chips, samples, outs), jnp.float32),
            pltpu.VMEM((chips - 1, samples, outs), bf16),
            pltpu.VMEM((chips - 1, samples, outs), bf16),
            dma((2,)),
            dma((inner - 1, outer)),
            dma((inner - 1, outer)),
            dma((outer - 1,)),
            dma((outer - 1,)),
            dma((chips,)),
            dma((chips,)),
            dma((chips,)),
            dma((chips,)),
            dma((chips,)),
            dma((chips,)),
            dma((chips - 1,)),
            dma((chips - 1,)),
        ],
        compiler_params=pltpu.CompilerParams(
            collective_id=1, has_side_effects=True, vmem_limit_bytes=50 * 2**20
        ),
        name="exchange",
    )(partial, top_in, top_bias[None, :], top_out)


def solution(mesh):
    return jax.shard_map(
        local,
        mesh=mesh,
        in_specs=(
            P(None, "gx", None),
            P(None, ("gx", "gy"), None, None),
            P(None, ("gx", "gy"), None),
            P(None, ("gx", "gy")),
            P(None, "gy"),
            P("gy"),
            P("gy", None),
        ),
        out_specs=P(("gx", "gy"), None),
        check_vma=False,
    )
```

profile of v0, /device:TPU:0, one launch (start us, length us, event | category | flops | bytes accessed | tf_op | source)
XLA Modules:
  0.0 96.4 jit_solution(11515558093826986845)
XLA Ops:
  0.0 1.5 %copy.10 = s32[4,256,16,1]{1,2,3,0:T(8,128)} copy(s32[4,256,16,1]{1,3,2,0:T(1,128)} %param.8) | data formatting | bytes 131072
  1.5 13.2 %sort_keys.1 = (s32[8,32,128]{2,1,0:T(8,128)}, s32[8,32,128]{2,1,0:T(8,128)}) custom-call(s32[4,16,256]{2,1,0:T(8,128)} %bitcast.9, s32[4,16,256]{2,1,0:T(8,128)} %bitcast.11, s32[4,256]{1,0:T(4,128)} %bag_ref.1), custom_call_target="tpu_custom_call" | custom-call | tf_op jit(solution)/shard_map/sort_keys/pallas_call | solution.py:376
  14.7 0.0 copy-start.1
  14.7 16.3 %pool.1.part_ref = bf16[8,256,512]{2,1,0:T(8,128)(2,1)} custom-call(s32[32768]{0:T(1024)} %bitcast.10, s32[8,32,128]{2,1,0:T(8,128)} %get-tuple-element.8.bags_ref, f32[4,8192,128]{2,1,0:T(8,128)} %table_ref.1), custom_call_target="tpu_custom_call" | custom-call | tf_op jit(solution)/shard_map/pool/pallas_call | solution.py:396
  31.0 0.0 copy-done.1
  31.0 0.0 copy-start
  31.0 1.6 %copy-done = bf16[8,256,512]{2,1,0:T(8,128)(2,1)S(1)} copy-done((bf16[8,256,512]{2,1,0:T(8,128)(2,1)S(1)}, bf16[8,256,512]{2,1,0:T(8,128)(2,1)}, u32[]{:S(2)}) %copy-start) | copy-done | bytes 2097176
  32.6 63.0 %exchange.1 = bf16[256,1024]{1,0:T(8,128)(2,1)S(1)} custom-call(bf16[8,256,512]{2,1,0:T(8,128)(2,1)S(1)} %copy-done, bf16[512,2048]{1,0:T(8,128)(2,1)} %top_in_ref.1, f32[1,2048]{1,0:T(1,128)S(1)} %bitcast.8, bf16[2048,1024]{1,0:T(8,128)(2,1)} %top_out_ref.1), custom_call_target="tpu_custom_call" | custom-call | tf_op jit(solution)/shard_map/exchange/pallas_call | solution.py:417
  95.6 0.8 copy.12
Async XLA Ops:
  14.7 16.3 %copy-start.1 = (f32[2048]{0:T(1024)S(1)}, f32[2048]{0:T(1024)}, u32[]{:S(2)}) copy-start(f32[2048]{0:T(1024)} %param.12) | copy-start | bytes 24580
  31.0 1.6 %copy-start = (bf16[8,256,512]{2,1,0:T(8,128)(2,1)S(1)}, bf16[8,256,512]{2,1,0:T(8,128)(2,1)}, u32[]{:S(2)}) copy-start(bf16[8,256,512]{2,1,0:T(8,128)(2,1)} %pool.1.part_ref) | copy-start | bytes 6291460
where the time goes:
time: 96.4 us
  Pallas kernels  92.5 us (96%)
  local copies, waits for them, and re-layouts  3.86 us (4%)
    pallas_call x1, Pallas kernels, local(): pl.pallas_call(exchange_kernel, out_shape=jax.ShapeDtypeStruct((samples,...  63 us
    pallas_call x1, Pallas kernels, local(): pl.pallas_call(pool_kernel, out_shape=jax.ShapeDtypeStruct((owners, sampl...  16.3 us
    pallas_call x1, Pallas kernels, local(): pl.pallas_call(functools.partial(sort_kernel, rows_dev), out_shape=(jax.S...  13.2 us
    unnamed x6, local copies, waits for them, and re-layouts  3.86 us

commit v1 on v0

v1 whole, which is shorter than its diff:
```python
import jax
import jax.numpy as jnp
from jax import lax
from jax.experimental import pallas as pl
from jax.experimental.pallas import tpu as pltpu
from jax.sharding import PartitionSpec as P

CHUNKS = 4
BIG = 2**31 - 1
MESH = pl.DeviceIdType.MESH


def log2(n):
    return n.bit_length() - 1


def bags_kernel(owner_ref, row_ref, bag_ref, table_ref, top_in_ref, bias_ref, top_out_ref, out_ref, mine, outbox, held, row_list, bag_list, rows, tab, stage, part_y, part_own, from_y, sum_y, from_z, feat, w_in, w_out, hid, kept, give, take, x_send, x_take, tsem, wsem, rsem, ksend, krec, ysend, yrec, zsend, zrec, gsend, grec, nsend, nrec, bsend, brec, fsend, frec):
    owners = held.shape[0]
    inner, outer = from_y.shape[0] + 1, sum_y.shape[0] + 1
    chips, chunks, rows_pair, width = feat.shape
    step = rows_pair // 2
    rows_dev = table_ref.shape[1]
    emb = table_ref.shape[2]
    me, mine_y = lax.axis_index("gx"), lax.axis_index("gy")
    z, y = me // inner, lax.rem(me, inner)
    chip, core = mine_y // 2, lax.rem(mine_y, 2)
    partner = {"gy": chip * 2 + 1 - core}

    def remote(src, dst, send, recv, device):
        return pltpu.make_async_remote_copy(
            src_ref=src, dst_ref=dst, send_sem=send, recv_sem=recv, device_id=device, device_id_type=MESH
        )

    def gx_at(dz, d):
        return {"gx": lax.rem(z + dz, outer) * inner + lax.rem(y + d, inner)}

    def chip_at(d):
        return {"gy": lax.rem(chip + d, chips) * 2 + core}

    barrier = pltpu.get_barrier_semaphore()
    peers = [gx_at(dz, d) for dz in range(outer) for d in range(inner) if dz or d]
    peers += [partner] + [chip_at(d) for d in range(1, chips)]
    for peer in peers:
        pl.semaphore_signal(barrier, inc=1, device_id=peer, device_id_type=MESH)
    tables_in = [
        pltpu.make_async_copy(table_ref.at[t], tab.at[pl.ds(t * rows_dev, rows_dev)], tsem.at[t])
        for t in range(table_ref.shape[0])
    ]
    weights_in = [
        pltpu.make_async_copy(top_in_ref, w_in, wsem.at[0]),
        pltpu.make_async_copy(top_out_ref, w_out, wsem.at[1]),
    ]
    for load in tables_in + weights_in:
        load.start()

    tables, bag_size, samples = owner_ref.shape
    owner = owner_ref[...]
    slot = lax.broadcasted_iota(jnp.int32, owner.shape, 1)
    sample = lax.broadcasted_iota(jnp.int32, owner.shape, 2)
    live = slot < bag_ref[...][:, None, :]
    key = jnp.where(live, (owner * samples + sample) * rows_dev + row_ref[...], BIG)
    count = bag_size * samples
    groups = count // 1024
    parts = []
    for t in range(tables):
        for c in range(samples // 128):
            for r in range(bag_size // 8):
                parts.append(key[t, r * 8 : r * 8 + 8, c * 128 : c * 128 + 128])
    lane = lax.broadcasted_iota(jnp.int32, (8, 128), 1)
    sub = lax.broadcasted_iota(jnp.int32, (8, 128), 0)
    place = lane * 8 + sub
    bits = log2(count)
    span = samples * rows_dev

    before = []
    for o in range(1, owners):
        for t in range(tables):
            tally = jnp.zeros((8, 128), jnp.int32)
            for g in range(groups):
                tally += (parts[t * groups + g] < o * span).astype(jnp.int32)
            before.append(jnp.sum(tally, axis=0, keepdims=True))
    before = jnp.sum(jnp.concatenate(before, axis=0), axis=1, keepdims=True)

    for k in range(1, bits + 1):
        for j in range(k - 1, -1, -1):
            d = 1 << j
            new = [None] * len(parts)
            for v in range(len(parts)):
                g = v % groups
                if d >= 1024:
                    gd = d // 1024
                    if g & gd:
                        continue
                    w = v + gd
                    low = jnp.minimum(parts[v], parts[w])
                    high = jnp.maximum(parts[v], parts[w])
                    up = ((g * 1024) >> k) & 1 == 0
                    new[v], new[w] = (low, high) if up else (high, low)
                    continue
                x = parts[v]
                if d < 8:
                    a, b = pltpu.roll(x, 8 - d, 0), pltpu.roll(x, d, 0)
                else:
                    s = d // 8
                    a, b = pltpu.roll(x, 128 - s, 1), pltpu.roll(x, s, 1)
                first = (place & d) == 0
                other = jnp.where(first, a, b)
                if (1 << k) >= 1024:
                    up = ((g * 1024) >> k) & 1 == 0
                    take_low = first if up else jnp.logical_not(first)
                else:
                    take_low = ((place >> k) ^ (place >> j)) & 1 == 0
                new[v] = jnp.where(take_low, jnp.minimum(x, other), jnp.maximum(x, other))
            parts = new
    stride = mine.shape[0] // tables
    for t in range(tables):
        for g in range(stride // 8):
            at = t * stride + g * 8
            mine[at : at + 8, :] = parts[t * groups + g] if g < groups else jnp.full((8, 128), BIG, jnp.int32)

    for o in range(owners):
        for t in range(tables):
            if o == 0:
                x = mine[t * stride : t * stride + 8, :]
            else:
                off = before[(o - 1) * tables + t, 0]
                low = off & 7

                def columns(first):
                    at = t * stride + ((first >> 7) << 3)
                    left = 128 - (first & 127)
                    turn = left & 127
                    p = pltpu.roll(mine[pl.ds(at, 8), :], turn, 1)
                    q = pltpu.roll(mine[pl.ds(at + 8, 8), :], turn, 1)
                    return pltpu.roll(jnp.where(lane < left, p, q), (8 - low) & 7, 0)

                x = jnp.where(sub < 8 - low, columns(off >> 3), columns((off >> 3) + 1))
            x = x - o * span
            ours = jnp.logical_and(x >= 0, x < span)
            outbox[o, t * 8 : t * 8 + 8, :] = jnp.where(ours, x, span)


    far_first = sorted(range(1, outer), key=lambda d: -min(d, outer - d)) + [0]
    slots = [(dz, d) for dz in far_first for d in [*range(1, inner), 0]]
    pl.semaphore_wait(barrier, len(peers))
    sends, key_in = [], {}
    for k, (dz, d) in enumerate(slots):
        if dz or d:
            to = gx_at(outer - dz, inner - d)
            key_in[k] = remote(outbox.at[to["gx"]], held.at[k], ksend.at[k], krec.at[k], to)
            key_in[k].start()
            sends.append(key_in[k])

    row_copies = {}

    def prepare(k):
        if k in key_in:
            key_in[k].wait_recv()
        for t in range(tables):
            at = pl.ds(t * 8, 8)
            x = held[k, at, :] if k in key_in else outbox[me, at, :]
            row_list[k, :, t : t + 1, :] = ((x & (rows_dev - 1)) + t * rows_dev)[:, None, :]
            bag_list[k, at, :] = x >> log2(rows_dev)
        row_copies[k] = [
            pltpu.make_async_copy(row_list.at[k, u], rows[u].at[pl.ds(k * tables, tables)], rsem.at[k, u])
            for u in range(8)
        ]
        for copy in row_copies[k]:
            copy.start()

    lanes = 2 * bag_size * samples // owners // 8
    if lanes < 128:
        stage[...] = jnp.zeros_like(stage)
    bag_index = lax.broadcasted_iota(jnp.int32, (samples, 128), 0)
    halves = 2
    some = tables // halves

    def pool(k, h, part):
        @pl.loop(0, some * (lanes // 8))
        def _(i):
            local = i // (lanes // 8)
            first = lax.rem(i, lanes // 8) * 8
            line = k * tables + h * some + local
            for q in range(8):
                for u in range(8):
                    row = rows[u][line, first + q]
                    stage[pl.ds(local * 1024 + first + u * 128 + q, 1), :] = tab[pl.ds(row, 1), :]

        for local in range(some):
            t = h * some + local
            picks = []
            for u in range(8):
                bag = bag_list[k, t * 8 + u : t * 8 + u + 1, :]
                picks.append(jnp.where(bag_index == bag, 1.0, 0.0).astype(jnp.bfloat16))
            picked = stage[local * 1024 : local * 1024 + 1024, :].astype(jnp.bfloat16)
            total = jnp.dot(jnp.concatenate(picks, axis=1), picked, preferred_element_type=jnp.float32)
            part[:, t * emb : (t + 1) * emb] = total.astype(part.dtype)

    y_in, z_in = {}, {}

    def along_z(dz, n, at):
        total = part_own[dz, at[0], at[1]].astype(jnp.float32)
        for d in range(1, inner):
            total += from_y[d - 1, dz, at[0], at[1]].astype(jnp.float32)
        sum_y[dz - 1, at[0], at[1]] = total.astype(sum_y.dtype)
        z_in[dz, n] = remote(
            sum_y.at[dz - 1, at[0], at[1]],
            from_z.at[dz - 1, at[0], at[1]],
            zsend.at[dz - 1, n],
            zrec.at[dz - 1, n],
            gx_at(dz, 0),
        )
        z_in[dz, n].start()
        sends.append(z_in[dz, n])

    def half_of(h):
        return pl.ds(h * width // halves, width // halves)

    def chunk_of(q):
        return pl.ds(q * step, step)

    whole = pl.ds(0, width)
    last = far_first[outer - 2]

    def z_event(dz, n):
        if dz == last:
            for h in range(halves):
                for d in range(1, inner):
                    y_in[dz, d, h].wait_recv()
            for q in range(chunks):
                along_z(dz, q, (chunk_of(q), whole))
        else:
            for d in range(1, inner):
                y_in[dz, d, n].wait_recv()
            along_z(dz, n, (pl.ds(0, samples), half_of(n)))

    due = {}
    waits = [(0, 2), (1, 3)]
    for i, dz in enumerate(far_first[: outer - 1]):
        end = (i + 1) * inner * halves
        if dz == last:
            due.setdefault(min(end + 3, len(slots) * halves), []).append((dz, 0))
        else:
            for n in range(halves):
                due.setdefault(min(end + waits[min(i, 1)][n], len(slots) * halves), []).append((dz, n))

    prepare(0)
    prepare(1)
    for load in tables_in:
        load.wait()
    done = 0
    for k, (dz, d) in enumerate(slots):
        if k + 2 < len(slots):
            prepare(k + 2)
        for copy in row_copies[k]:
            copy.wait()
        part = part_y.at[d - 1, dz] if d else part_own.at[dz]
        for h in range(halves):
            pool(k, h, part)
            if d:
                y_in[dz, d, h] = remote(
                    part.at[:, half_of(h)],
                    from_y.at[d - 1, dz, :, half_of(h)],
                    ysend.at[d - 1, dz, h],
                    yrec.at[d - 1, dz, h],
                    gx_at(0, d),
                )
                y_in[dz, d, h].start()
                sends.append(y_in[dz, d, h])
            done += 1
            for event in due.get(done, []):
                z_event(*event)

    far, near = {}, {}
    for d in range(1, inner):
        for h in range(halves):
            y_in[0, d, h].wait_recv()
    for dz in range(1, outer):
        if dz != last:
            for n in range(halves):
                z_in[dz, n].wait_recv()
    for q in range(chunks):
        z_in[last, q].wait_recv()
        at = chunk_of(q)
        total = part_own[0, at, :].astype(jnp.float32)
        for d in range(1, inner):
            total += from_y[d - 1, 0, at, :].astype(jnp.float32)
        for dz in range(1, outer):
            total += from_z[dz - 1, at, :].astype(jnp.float32)
        feat[0, q, 0:step, :] = total.astype(feat.dtype)
        for d in range(1, chips):
            far[d, q] = remote(
                feat.at[0, q, pl.ds(0, step)],
                feat.at[chips - d, q, pl.ds(0, step)],
                gsend.at[d, q],
                grec.at[chips - d, q],
                chip_at(d),
            )
            far[d, q].start()
        near[0, q] = remote(
            feat.at[0, q, pl.ds(0, step)], feat.at[0, q, pl.ds(step, step)], nsend.at[0, q], nrec.at[0, q], partner
        )
        near[0, q].start()

    for load in weights_in:
        load.wait()
    hidden, outs = w_in.shape[1], w_out.shape[1]
    in_tile, out_tile = min(1024, hidden), min(512, outs)
    back, far_out = {}, {}

    def scores(d, q):
        @pl.loop(0, hidden // in_tile)
        def _(i):
            cols = pl.ds(pl.multiple_of(i * in_tile, in_tile), in_tile)
            pre = jnp.dot(feat[d, q], w_in[:, cols], preferred_element_type=jnp.float32) + bias_ref[:, cols]
            hid[:, cols] = jnp.maximum(pre, 0.0).astype(hid.dtype)

        @pl.loop(0, outs // out_tile)
        def _(i):
            cols = pl.ds(pl.multiple_of(i * out_tile, out_tile), out_tile)
            score = jnp.dot(hid[...], w_out[:, cols], preferred_element_type=jnp.float32)
            kept[d, q, :, cols] = score[0:step]
            give[d, q, :, cols] = score[step : 2 * step].astype(give.dtype)

        back[d, q] = remote(give.at[d, q], take.at[d, q], bsend.at[d, q], brec.at[d, q], partner)
        back[d, q].start()

    def forward(d, q):
        far[chips - d, q].wait_recv()
        near[d, q] = remote(
            feat.at[d, q, pl.ds(0, step)], feat.at[d, q, pl.ds(step, step)], nsend.at[d, q], nrec.at[d, q], partner
        )
        near[d, q].start()

    def along_x(d, q):
        back[d, q].wait_recv()
        total = kept[d, q] + take[d, q].astype(jnp.float32)
        x_send[d - 1, q] = total.astype(x_send.dtype)
        far_out[d, q] = remote(
            x_send.at[d - 1, q], x_take.at[d - 1, q], fsend.at[d - 1, q], frec.at[d - 1, q], chip_at(d)
        )
        far_out[d, q].start()

    work = [(d, q) for q in range(chunks) for d in range(1, chips)]
    forward(*work[0])
    near[0, 0].wait_recv()
    scores(0, 0)
    for i, (d, q) in enumerate(work):
        if i + 1 < len(work):
            forward(*work[i + 1])
        near[d, q].wait_recv()
        scores(d, q)
        if i:
            along_x(*work[i - 1])
    rest = list(range(1, chunks))
    near[0, rest[0]].wait_recv()
    along_x(*work[-1])
    for q in rest:
        if q != rest[0]:
            near[0, q].wait_recv()
        scores(0, q)
    for q in range(chunks):
        back[0, q].wait_recv()
        total = kept[0, q] + take[0, q].astype(jnp.float32)
        for d in range(1, chips):
            far_out[d, q].wait_recv()
            total += x_take[d - 1, q].astype(jnp.float32)
        out_ref[chunk_of(q), :] = total.astype(out_ref.dtype)

    for group in (far, near, back, far_out):
        sends += list(group.values())
    for copy in sends:
        copy.wait_send()


def local(table, lookup_owner, lookup_row, bag_length, top_in, top_bias, top_out):
    owners = lax.axis_size("gx")
    tables, samples, bag_size = lookup_row.shape
    rows_dev = table.shape[1]
    emb = table.shape[2]
    count = samples * bag_size
    assert 2 * count // owners <= 1024
    inner = max(1, owners // 4)
    outer = owners // inner
    chips = lax.axis_size("gy") // 2
    width = tables * emb
    hidden, outs = top_out.shape
    step = samples // CHUNKS
    bf16, f32, i32, dma = jnp.bfloat16, jnp.float32, jnp.int32, pltpu.SemaphoreType.DMA
    vmem = pl.BlockSpec(memory_space=pltpu.VMEM)
    anywhere = pl.BlockSpec(memory_space=pl.ANY)
    windows = pltpu.VMEM((owners, tables * 8, 128), i32)
    pieces = max(CHUNKS, 2)
    pairs = [dma((owners,))] * 2 + [dma((inner - 1, outer, 2))] * 2 + [dma((outer - 1, pieces))] * 2
    pairs += [dma((chips, CHUNKS))] * 6 + [dma((chips - 1, CHUNKS))] * 2
    return pl.pallas_call(
        bags_kernel,
        out_shape=jax.ShapeDtypeStruct((samples, outs), bf16),
        in_specs=[vmem, vmem, vmem, anywhere, anywhere, vmem, anywhere],
        out_specs=vmem,
        scratch_shapes=[
            pltpu.VMEM((tables * (count // 128 + 16), 128), i32),
            windows,
            windows,
            pltpu.VMEM((owners, 8, tables, 128), i32),
            windows,
            [pltpu.SMEM((owners * tables, 128), i32) for _ in range(8)],
            pltpu.VMEM((tables * rows_dev, emb), f32),
            pltpu.VMEM((tables // 2 * 1024, emb), f32),
            pltpu.VMEM((inner - 1, outer, samples, width), bf16),
            pltpu.VMEM((outer, samples, width), bf16),
            pltpu.VMEM((inner - 1, outer, samples, width), bf16),
            pltpu.VMEM((outer - 1, samples, width), bf16),
            pltpu.VMEM((outer - 1, samples, width), bf16),
            pltpu.VMEM((chips, CHUNKS, 2 * step, width), bf16),
            pltpu.VMEM((width, hidden), bf16),
            pltpu.VMEM((hidden, outs), bf16),
            pltpu.VMEM((2 * step, hidden), bf16),
            pltpu.VMEM((chips, CHUNKS, step, outs), f32),
            pltpu.VMEM((chips, CHUNKS, step, outs), bf16),
            pltpu.VMEM((chips, CHUNKS, step, outs), bf16),
            pltpu.VMEM((chips - 1, CHUNKS, step, outs), bf16),
            pltpu.VMEM((chips - 1, CHUNKS, step, outs), bf16),
            dma((tables,)),
            dma((2,)),
            dma((owners, 8)),
            *pairs,
        ],
        compiler_params=pltpu.CompilerParams(
            collective_id=0, has_side_effects=True, vmem_limit_bytes=60 * 2**20
        ),
        name="bags",
    )(
        jnp.transpose(lookup_owner[..., 0], (0, 2, 1)),
        jnp.transpose(lookup_row, (0, 2, 1)),
        bag_length,
        table,
        top_in,
        top_bias[None, :],
        top_out,
    )


def solution(mesh):
    return jax.shard_map(
        local,
        mesh=mesh,
        in_specs=(
            P(None, "gx", None),
            P(None, ("gx", "gy"), None, None),
            P(None, ("gx", "gy"), None),
            P(None, ("gx", "gy")),
            P(None, "gy"),
            P("gy"),
            P("gy", None),
        ),
        out_specs=P(("gx", "gy"), None),
        check_vma=False,
    )
```

time: 96.4 us -> 78 us (0.81)
  Pallas kernels: 92.5 us -> 74.4 us
    pallas_call x3 -> x1, Pallas kernels: 92.5 us -> 74.4 us  [local(): pl.pallas_call(bags_kernel, out_shape=jax.ShapeDtypeStruct((samples, outs...]
    unnamed x6 -> x2, local copies, waits for them, and re-layouts: 3.86 us -> 3.34 us
where the time goes in v1:
time: 78 us; the launch traced here: 77.8 us
  Pallas kernels  74.4 us (95%)
  local copies, waits for them, and re-layouts  3.34 us (4%)
    pallas_call x1, Pallas kernels, local(): pl.pallas_call(bags_kernel, out_shape=jax.ShapeDtypeStruct((samples, outs...  74.4 us
    unnamed x2, local copies, waits for them, and re-layouts  3.34 us

profile of v1, /device:TPU:0, one launch (start us, length us, event | category | flops | bytes accessed | tf_op | source)
XLA Modules:
  0.0 77.8 jit_solution(17706612457418718546)
XLA Ops:
  0.0 1.5 %copy.10 = s32[4,256,16,1]{1,2,3,0:T(8,128)} copy(s32[4,256,16,1]{1,3,2,0:T(1,128)} %param.8) | data formatting | bytes 131072
  1.5 74.4 %bags.1 = bf16[256,1024]{1,0:T(8,128)(2,1)} custom-call(s32[4,16,256]{2,1,0:T(8,128)} %bitcast.7, s32[4,16,256]{2,1,0:T(8,128)} %bitcast.8, s32[4,256]{1,0:T(4,128)} %bag_ref.1, f32[4,8192,128]{2,1,0:T(8,128)} %table_ref.1, bf16[512,2048]{1,0:T(8,128)(2,1)} %top_in_ref.1, f32[1,2048]{1,0:T(1,128)} %bitcast.9, bf16[2048,1024]{1,0:T(8,128)(2,1)} %top_out_ref.1), custom_call_target="tpu_custom_call" | custom-call | tf_op jit(solution)/shard_map/bags/pallas_call | solution.py:396
  75.9 1.9 %copy.12 = bf16[256,1024]{1,0:T(8,128)(2,1)} copy(bf16[256,1024]{1,0:T(8,128)(2,1)} %bags.1) | data formatting | bytes 1048576

commit v2 on v1

--- a/solution.py
+++ b/solution.py
@@ -43,7 +43,7 @@
     for peer in peers:
         pl.semaphore_signal(barrier, inc=1, device_id=peer, device_id_type=MESH)
     tables_in = [
-        pltpu.make_async_copy(table_ref.at[t], tab.at[pl.ds(t * rows_dev, rows_dev)], tsem.at[t])
+        pltpu.make_async_copy(table_ref.at[t], tab[t], tsem.at[t])
         for t in range(table_ref.shape[0])
     ]
     weights_in = [
@@ -53,8 +53,8 @@
     for load in tables_in + weights_in:
         load.start()
 
-    tables, bag_size, samples = owner_ref.shape
-    owner = owner_ref[...]
+    tables, bag_size, samples = row_ref.shape
+    owner = owner_ref[:, :, 0, :]
     slot = lax.broadcasted_iota(jnp.int32, owner.shape, 1)
     sample = lax.broadcasted_iota(jnp.int32, owner.shape, 2)
     live = slot < bag_ref[...][:, None, :]
@@ -159,7 +159,7 @@
         for t in range(tables):
             at = pl.ds(t * 8, 8)
             x = held[k, at, :] if k in key_in else outbox[me, at, :]
-            row_list[k, :, t : t + 1, :] = ((x & (rows_dev - 1)) + t * rows_dev)[:, None, :]
+            row_list[k, :, t : t + 1, :] = (x & (rows_dev - 1))[:, None, :]
             bag_list[k, at, :] = x >> log2(rows_dev)
         row_copies[k] = [
             pltpu.make_async_copy(row_list.at[k, u], rows[u].at[pl.ds(k * tables, tables)], rsem.at[k, u])
@@ -176,15 +176,17 @@
     some = tables // halves
 
     def pool(k, h, part):
-        @pl.loop(0, some * (lanes // 8))
-        def _(i):
-            local = i // (lanes // 8)
-            first = lax.rem(i, lanes // 8) * 8
-            line = k * tables + h * some + local
-            for q in range(8):
-                for u in range(8):
-                    row = rows[u][line, first + q]
-                    stage[pl.ds(local * 1024 + first + u * 128 + q, 1), :] = tab[pl.ds(row, 1), :]
+        for local in range(some):
+            t = h * some + local
+            line = k * tables + t
+            lists = [rows[u].at[line] for u in range(8)]
+
+            @pl.loop(0, lanes // 8)
+            def _(i):
+                for q in range(8):
+                    for u in range(8):
+                        row = lists[u][i * 8 + q]
+                        stage[pl.ds(local * 1024 + i * 8 + u * 128 + q, 1), :] = tab[t][pl.ds(row, 1), :]
 
         for local in range(some):
             t = h * some + local
@@ -246,8 +248,6 @@
 
     prepare(0)
     prepare(1)
-    for load in tables_in:
-        load.wait()
     done = 0
     for k, (dz, d) in enumerate(slots):
         if k + 2 < len(slots):
@@ -256,6 +256,9 @@
             copy.wait()
         part = part_y.at[d - 1, dz] if d else part_own.at[dz]
         for h in range(halves):
+            if k == 0:
+                for t in range(h * some, (h + 1) * some):
+                    tables_in[t].wait()
             pool(k, h, part)
             if d:
                 y_in[dz, d, h] = remote(
@@ -405,7 +408,7 @@
             pltpu.VMEM((owners, 8, tables, 128), i32),
             windows,
             [pltpu.SMEM((owners * tables, 128), i32) for _ in range(8)],
-            pltpu.VMEM((tables * rows_dev, emb), f32),
+            [pltpu.VMEM((rows_dev, emb), f32) for _ in range(tables)],
             pltpu.VMEM((tables // 2 * 1024, emb), f32),
             pltpu.VMEM((inner - 1, outer, samples, width), bf16),
             pltpu.VMEM((outer, samples, width), bf16),
@@ -431,7 +434,7 @@
         ),
         name="bags",
     )(
-        jnp.transpose(lookup_owner[..., 0], (0, 2, 1)),
+        jnp.transpose(lookup_owner, (0, 2, 3, 1)),
         jnp.transpose(lookup_row, (0, 2, 1)),
         bag_length,
         table,

time: 78 us -> 69.8 us (0.89)
  Pallas kernels: 74.4 us -> 67.7 us
  local copies, waits for them, and re-layouts: 3.34 us -> 1.87 us
    pallas_call x1, Pallas kernels: 74.4 us -> 67.7 us  [local(): pl.pallas_call(bags_kernel, out_shape=jax.ShapeDtypeStruct((samples, outs...]
    unnamed x2 -> x1, local copies, waits for them, and re-layouts: 3.34 us -> 1.87 us
where the time goes in v2:
time: 69.8 us; the launch traced here: 69.6 us
  Pallas kernels  67.7 us (97%)
  local copies, waits for them, and re-layouts  1.87 us (3%)
    pallas_call x1, Pallas kernels, local(): pl.pallas_call(bags_kernel, out_shape=jax.ShapeDtypeStruct((samples, outs...  67.7 us
    unnamed x1, local copies, waits for them, and re-layouts  1.87 us

profile of v2, /device:TPU:0, one launch (start us, length us, event | category | flops | bytes accessed | tf_op | source)
XLA Modules:
  0.0 69.6 jit_solution(7403069105820763674)
XLA Ops:
  0.0 67.7 %bags.1 = bf16[256,1024]{1,0:T(8,128)(2,1)} custom-call(s32[4,16,1,256]{3,2,1,0:T(1,128)} %bitcast.3, s32[4,16,256]{2,1,0:T(8,128)} %bitcast.4, s32[4,256]{1,0:T(4,128)} %bag_ref.1, f32[4,8192,128]{2,1,0:T(8,128)} %table_ref.1, bf16[512,2048]{1,0:T(8,128)(2,1)} %top_in_ref.1, f32[1,2048]{1,0:T(1,128)} %bitcast.5, bf16[2048,1024]{1,0:T(8,128)(2,1)} %top_out_ref.1), custom_call_target="tpu_custom_call" | custom-call | tf_op jit(solution)/shard_map/bags/pallas_call | solution.py:399
  67.7 1.9 %copy.9 = bf16[256,1024]{1,0:T(8,128)(2,1)} copy(bf16[256,1024]{1,0:T(8,128)(2,1)} %bags.1) | data formatting | bytes 1048576

commit v3 on v2

--- a/solution.py
+++ b/solution.py
@@ -181,12 +181,12 @@
             line = k * tables + t
             lists = [rows[u].at[line] for u in range(8)]
 
-            @pl.loop(0, lanes // 8)
+            @pl.loop(0, lanes // 16)
             def _(i):
-                for q in range(8):
+                for q in range(16):
                     for u in range(8):
-                        row = lists[u][i * 8 + q]
-                        stage[pl.ds(local * 1024 + i * 8 + u * 128 + q, 1), :] = tab[t][pl.ds(row, 1), :]
+                        row = lists[u][i * 16 + q]
+                        stage[pl.ds(local * 1024 + i * 16 + u * 128 + q, 1), :] = tab[t][pl.ds(row, 1), :]
 
         for local in range(some):
             t = h * some + local

time: 69.8 us -> 68.7 us (0.984)
  Pallas kernels: 67.7 us -> 66.6 us
    pallas_call x1, Pallas kernels: 67.7 us -> 66.6 us  [local(): pl.pallas_call(bags_kernel, out_shape=jax.ShapeDtypeStruct((samples, outs...]
where the time goes in v3:
time: 68.7 us; the launch traced here: 68.5 us
  Pallas kernels  66.6 us (97%)
  local copies, waits for them, and re-layouts  1.87 us (3%)
    pallas_call x1, Pallas kernels, local(): pl.pallas_call(bags_kernel, out_shape=jax.ShapeDtypeStruct((samples, outs...  66.6 us
    unnamed x1, local copies, waits for them, and re-layouts  1.87 us

profile of v3, /device:TPU:0, one launch (start us, length us, event | category | flops | bytes accessed | tf_op | source)
XLA Modules:
  0.0 68.5 jit_solution(12620482157331056804)
XLA Ops:
  0.0 66.6 %bags.1 = bf16[256,1024]{1,0:T(8,128)(2,1)} custom-call(s32[4,16,1,256]{3,2,1,0:T(1,128)} %bitcast.3, s32[4,16,256]{2,1,0:T(8,128)} %bitcast.4, s32[4,256]{1,0:T(4,128)} %bag_ref.1, f32[4,8192,128]{2,1,0:T(8,128)} %table_ref.1, bf16[512,2048]{1,0:T(8,128)(2,1)} %top_in_ref.1, f32[1,2048]{1,0:T(1,128)} %bitcast.5, bf16[2048,1024]{1,0:T(8,128)(2,1)} %top_out_ref.1), custom_call_target="tpu_custom_call" | custom-call | tf_op jit(solution)/shard_map/bags/pallas_call | solution.py:399
  66.6 1.9 %copy.9 = bf16[256,1024]{1,0:T(8,128)(2,1)} copy(bf16[256,1024]{1,0:T(8,128)(2,1)} %bags.1) | data formatting | bytes 1048576
